TPU v7x, 16 devices: a 4x2x1 block of a 4x4x8 slice. The times are simulated.
16 devices in a mesh: dp: 2 (over y, z), sp: 8 (over x, core).
Axes of the slice: x: 4, y: 2, z: 1, core: 2. Of those that a mesh axis runs over, the one named last changes fastest.
The devices are a block of a 4x4x8 slice.
Arguments:
- q: bfloat16 [64, 8, 256], P('dp'), parts along dimension 0
- k: bfloat16 [64, 4096, 8, 256], P('dp', 'sp'), parts along dimension 0
- v: bfloat16 [64, 4096, 8, 256], P('dp', 'sp'), parts along dimension 0
Outputs:
- q: bfloat16 [64, 8, 256], P('dp'), parts along dimension 0
There are 2 independent parts. A program takes and returns all parts, laid end to end along the dimension named above; each array names one.
All inputs are finite; a program needn't handle non-finite values.
Results may differ from a plain program's by a relative error of at most 0.012.
Values are sent between devices in bfloat16 or wider.
A program may use at most 768 MiB of HBM per device.

v0:
```python
import jax
import jax.numpy as jnp
from jax import lax
from jax.sharding import PartitionSpec as P


def einsum(form, a, b):
    return jnp.einsum(form, a.astype(jnp.float32), b.astype(jnp.float32))


def part_of(q, k, v):
    grouped = q.reshape(q.shape[0], k.shape[2], -1, q.shape[2])
    scores = einsum("bgsd,bugd->bgsu", grouped, k) * q.shape[2] ** -0.5
    high = jnp.max(scores, -1, keepdims=True)
    weights = jnp.exp(scores - high)
    seen = einsum("bgsu,bugd->bgsd", weights.astype(jnp.bfloat16), v)
    return jnp.concatenate([seen, jnp.sum(weights, -1, keepdims=True), high], -1)


def together(parts):
    seen, total, high = parts[..., :-2], parts[..., -2:-1], parts[..., -1:]
    scale = jnp.exp(high - jnp.max(high, 0))
    return (jnp.sum(seen * scale, 0) / jnp.sum(total * scale, 0)).astype(jnp.bfloat16)


def solution(mesh):
    def step(q, k, v):
        return together(lax.all_gather(part_of(q, k, v), "sp")).reshape(q.shape)

    return jax.shard_map(
        step,
        mesh=mesh,
        in_specs=(P("dp", None, None), P("dp", "sp", None, None), P("dp", "sp", None, None)),
        out_specs=P("dp", None, None),
        check_vma=False,
    )
```

profile of v0, /device:TPU:113, one launch (start us, length us, event | category | flops | bytes accessed | tf_op | source)
XLA Modules:
  0.0 114.6 jit_solution(12649812764052740574)
XLA Ops:
  6.5 0.0 all-gather.3.cloned.1.call-start
  6.6 31.9 %fusion.2 = f32[32,8,1,512]{3,2,1,0:T(1,128)S(1)} fusion(bf16[32,512,8,256]{3,2,1,0:T(8,128)(2,1)} %param.4, bf16[32,8,256,1]{2,1,0,3:T(8,128)(2,1)} %bitcast.26), kind=kOutput, calls=%fused_computation.2 | convolution fusion | flops 67108864 | bytes 67764224 | tf_op jit(solution)/shard_map/bgsd,bugd->bgsu/dot_general | solution.py:8
  38.4 0.1 fusion.9
  38.5 0.2 fusion.10
  38.8 32.5 %fusion = f32[32,8,1,256]{3,2,1,0:T(1,128)S(1)} fusion(bf16[32,512,8,256]{3,2,1,0:T(8,128)(2,1)} %param.5, bf16[32,8,512,1]{2,1,0,3:T(8,128)(2,1)S(1)} %get-tuple-element.7), kind=kOutput, calls=%fused_computation | convolution fusion | flops 67108864 | bytes 67633152 | tf_op jit(solution)/shard_map/bgsu,bugd->bgsd/dot_general | solution.py:8
  71.3 0.3 copy.23
  71.5 0.3 copy.22
  71.8 0.8 pad_maximum_fusion
  72.6 0.1 all-gather.3.cloned.1.call-update
  72.7 26.9 %all-gather.3.cloned.1.call-done = f32[256,8,1,258]{3,1,2,0:T(8,128)} async-done(((f32[32,8,1,258]{3,1,2,0:T(8,128)}), f32[256,8,1,258]{3,1,2,0:T(8,128)}) %all-gather.3.cloned.1.call-update) | async-done | bytes 2113552 | tf_op jit(solution)/shard_map/all_gather | solution.py:28
  99.6 1.6 %slice_reduce_fusion = f32[32,8]{1,0:T(8,128)S(1)} fusion(f32[8,32,8,1,258]{4,2,1,0,3:T(8,128)} %bitcast.22), kind=kLoop, calls=%fused_computation.9 | loop fusion | flops 1792 | bytes 9216 | tf_op jit(solution)/shard_map/reduce_max | solution.py:22
  101.2 2.3 %fusion.5 = (f32[32,8]{1,0:T(8,128)S(1)}, f32[8,32,8,1,1]{4,2,1,0,3:T(8,128)S(1)}) fusion(f32[8,32,8,1,258]{4,2,1,0,3:T(8,128)} %bitcast.23, f32[32,8]{1,0:T(8,128)S(1)} %slice_reduce_fusion), kind=kLoop, calls=%fused_computation.7 | loop fusion | flops 5888 | bytes 26624 | tf_op jit(solution)/shard_map/reduce_sum | solution.py:23
  103.5 1.6 %copy.36 = f32[8,32,8,1,1]{2,1,0,3,4:T(8,128)S(1)} copy(f32[8,32,8,1,1]{4,2,1,0,3:T(8,128)S(1)} %get-tuple-element.6) | data formatting | bytes 16384 | tf_op jit(solution)/shard_map/mul | solution.py:23
  105.1 2.0 %fusion.4 = f32[32,8,256]{2,1,0:T(8,128)S(1)} fusion(f32[8,32,8,1,258]{4,2,1,0,3:T(8,128)} %bitcast.24, f32[8,32,8]{2,1,0:T(8,128)S(1)} %bitcast.27), kind=kLoop, calls=%fused_computation.5 | loop fusion | flops 983040 | bytes 2367488 | tf_op jit(solution)/shard_map/reduce_sum | solution.py:23
  107.0 0.8 divide_convert_fusion
  (1 shorter events, 0.0 us)
Async XLA Ops:
  6.5 93.0 %all-gather.3.cloned.1.call-start = ((), (), s32[]{:S(2)}) async-start(), calls=%async_computation | async-start | bytes 3538944 | tf_op jit(solution)/shard_map/all_gather | solution.py:28
Sparse Core Ops, SparseCore 0:
  72.8 26.7 all-gather.2
where the time goes:
time: 115 us
  matrix products  64.3 us (56%)
  waiting for transfers between devices  26.9 us (23%)
  between operations  13.5 us (12%)
  other arithmetic  7.84 us (7%)
  local copies, waits for them, and re-layouts  2.1 us (2%)
    dot_general x2, matrix products, einsum(): return jnp.einsum(form, a.astype(jnp.float32), b.astype(jnp.float32))  64.3 us
    all_gather x1, waiting for transfers between devices, step(): return together(lax.all_gather(part_of(q, k, v), 'sp')).reshape(q.shape)  26.9 us
  transfers between devices with their start and end apart: 1, of which 1 were waited for; matrix products, arithmetic and copies ran while one was open for 0% of the time, Pallas kernels for 0%

commit v1 on v0

v1 whole, which is shorter than its diff:
```python
import functools

import jax
import jax.numpy as jnp
from jax import lax
from jax.experimental import pallas as pl
from jax.experimental.pallas import tpu as pltpu
from jax.sharding import PartitionSpec as P

SLOTS = 4
GROUP = 2
MESH = pl.DeviceIdType.MESH


def iotas():
    return lax.broadcasted_iota(jnp.int32, (8, 128), 1), lax.broadcasted_iota(jnp.int32, (8, 128), 0)


def scores_of(q, k_ref):
    lane, sub = iotas()
    spread = jnp.concatenate([q] * 16, 0)
    full = lax.dot_general(k_ref[...], spread, (((1,), (1,)), ((), ())), preferred_element_type=jnp.float32)
    full = full.reshape(-1, 16, 8, 128)
    out = []
    for r in range(full.shape[0]):
        level = [full[r, i] for i in range(16)]
        bit = 8
        while len(level) > 1:
            level = [jnp.where((lane & bit) != 0, level[i + 1], level[i]) for i in range(0, len(level), 2)]
            bit *= 2
        out.append(jnp.sum(jnp.where((lane & 7) == sub, level[0], 0.0), 0, keepdims=True))
    return jnp.concatenate(out, 0)


def fold(x, op):
    turned = [x] + [pltpu.roll(x, s, 1) for s in range(8, 128, 8)]
    while len(turned) > 1:
        turned = [op(turned[i], turned[i + 1]) for i in range(0, len(turned), 2)]
    return turned[0]


def kernel(q_ref, k_ref, v_ref, o_ref, k_buf, v_buf, gathered, sums, k_sem, v_sem, send_sem, recv_sem, send_sum, recv_sum):
    batch = k_ref.shape[0]
    n = lax.axis_size("sp")
    me = lax.axis_index("sp")
    lane, sub = iotas()
    diag = (lane & 7) == sub

    def k_copy(b, slot):
        return pltpu.make_async_copy(k_ref.at[b], k_buf.at[slot], k_sem.at[slot])

    def v_copy(b, slot):
        return pltpu.make_async_copy(v_ref.at[b], v_buf.at[slot], v_sem.at[slot])

    k_copy(0, 0).start()
    k_copy(1, 1).start()
    for b in range(2, SLOTS):
        v_copy(b - 2, b - 2).start()
        k_copy(b, b).start()
    v_copy(SLOTS - 2, SLOTS - 2).start()
    v_copy(SLOTS - 1, SLOTS - 1).start()

    barrier = pltpu.get_barrier_semaphore()
    for step in range(1, n):
        pl.semaphore_signal(barrier, inc=1, device_id={"sp": lax.rem(me + step, n)}, device_id_type=MESH)

    def score(b, slot):
        return scores_of(q_ref[b], k_buf.at[slot]) * k_ref.shape[2] ** -0.5

    def soften(s):
        high = fold(jnp.max(s, 0, keepdims=True), jnp.maximum)
        p = jnp.exp(s - high)
        total = fold(jnp.sum(p, 0, keepdims=True), jnp.add)
        return p, jnp.where(lane[:1] < 64, high, total)

    def weigh(p, slot):
        big = [jnp.where(diag, jnp.broadcast_to(p[r:r + 1], (8, 128)), 0.0) for r in range(p.shape[0])]
        return jnp.dot(jnp.concatenate(big, 1).astype(jnp.bfloat16), v_buf[slot], preferred_element_type=jnp.float32)

    def copies(first, count, which, owner, step):
        peer = {"sp": lax.rem(me + step, n)}
        block, block_sums = gathered.at[owner, pl.ds(first, count)], sums.at[owner, pl.ds(first, count)]
        return (
            pltpu.make_async_remote_copy(block, block, send_sem.at[which, step], recv_sem.at[which, owner], device_id=peer, device_id_type=MESH),
            pltpu.make_async_remote_copy(block_sums, block_sums, send_sum.at[which, step], recv_sum.at[which, owner], device_id=peer, device_id_type=MESH),
        )

    def send(first, count, which):
        for step in range(1, n):
            for copy in copies(first, count, which, me, step):
                copy.start()

    def received(first, count, which):
        for step in range(1, n):
            for copy in copies(first, count, which, lax.rem(me + step, n), step):
                copy.wait_recv()

    def sent(first, count, which):
        for step in range(1, n):
            for copy in copies(first, count, which, me, step):
                copy.wait_send()

    def combine(b):
        rows = jnp.concatenate([sums[d, b] for d in range(n)], 0)
        high = jnp.max(rows, 0, keepdims=True)
        scale = jnp.exp(rows - high)
        total = jnp.sum(pltpu.roll(rows, 64, 1) * scale, 0, keepdims=True)
        scale = scale / total
        result = jnp.zeros(o_ref.shape[1:], jnp.float32)
        for d in range(n):
            column = jnp.sum(jnp.where(lane == sub, jnp.broadcast_to(scale[d:d + 1], (8, 128)), 0.0), 1, keepdims=True)
            result += gathered[d, b].astype(jnp.float32) * column
        o_ref[b] = result.astype(o_ref.dtype)

    main = batch - 2

    k_copy(0, 0).wait()
    s0 = score(0, 0)
    k_copy(1, 1).wait()
    p0, row = soften(s0)
    s1 = score(1, 1)
    sums[me, 0] = row
    for b in range(2):
        k_copy(b + SLOTS, b).start()
    pl.semaphore_wait(barrier, n - 1)

    def body(b, carry):
        s, p = carry
        slot, k_slot = lax.rem(b, SLOTS), lax.rem(b + 2, SLOTS)
        v_copy(b, slot).wait()
        k_copy(b + 2, k_slot).wait()
        gathered[me, b] = weigh(p, slot).astype(jnp.bfloat16)
        s_next = score(b + 2, k_slot)
        p_next, row = soften(s)
        sums[me, b + 1] = row

        @pl.when(b + SLOTS < batch)
        def _():
            v_copy(b + SLOTS, slot).start()

        @pl.when(b + 2 + SLOTS < batch)
        def _():
            k_copy(b + 2 + SLOTS, k_slot).start()

        @pl.when(lax.rem(b, GROUP) == GROUP - 1)
        def _():
            send(b - (GROUP - 1), GROUP, 0)

        return s_next, p_next

    s, p = lax.fori_loop(0, batch - 2, body, (s1, p0))
    v_copy(main, main % SLOTS).wait()
    gathered[me, main] = weigh(p, main % SLOTS).astype(jnp.bfloat16)
    p, row = soften(s)
    last = batch - 1
    sums[me, last] = row
    send(main, 1, 1)
    v_copy(last, last % SLOTS).wait()
    gathered[me, last] = weigh(p, last % SLOTS).astype(jnp.bfloat16)
    send(last, 1, 2)

    received(0, main, 0)

    def finish(i, _):
        for j in range(5):
            combine(i * 5 + j)
        return 0

    lax.fori_loop(0, main // 5, finish, 0)
    received(main, 1, 1)
    combine(main)
    received(last, 1, 2)
    combine(last)
    sent(0, main, 0)
    sent(main, 1, 1)
    sent(last, 1, 2)


def solution(mesh):
    n = mesh.shape["sp"]

    def step(q, k, v):
        b, u, h, d = k.shape
        rows = u * h
        return pl.pallas_call(
            kernel,
            out_shape=jax.ShapeDtypeStruct((b, h, d), jnp.bfloat16),
            in_specs=[pl.BlockSpec(memory_space=pltpu.VMEM), pl.BlockSpec(memory_space=pl.ANY), pl.BlockSpec(memory_space=pl.ANY)],
            out_specs=pl.BlockSpec(memory_space=pltpu.VMEM),
            scratch_shapes=[
                pltpu.VMEM((SLOTS, rows, d), jnp.bfloat16),
                pltpu.VMEM((SLOTS, rows, d), jnp.bfloat16),
                pltpu.VMEM((n, b, h, d), jnp.bfloat16),
                pltpu.VMEM((n, b, 1, 128), jnp.float32),
                pltpu.SemaphoreType.DMA((SLOTS,)),
                pltpu.SemaphoreType.DMA((SLOTS,)),
                pltpu.SemaphoreType.DMA((3, n)),
                pltpu.SemaphoreType.DMA((3, n)),
                pltpu.SemaphoreType.DMA((3, n)),
                pltpu.SemaphoreType.DMA((3, n)),
            ],
            name="decode",
            compiler_params=pltpu.CompilerParams(collective_id=0, has_side_effects=True, vmem_limit_bytes=60 * 1024 * 1024),
        )(q, k.reshape(b, rows, d), v.reshape(b, rows, d))

    return jax.shard_map(
        step,
        mesh=mesh,
        in_specs=(P("dp", None, None), P("dp", "sp", None, None), P("dp", "sp", None, None)),
        out_specs=P("dp", None, None),
        check_vma=False,
    )
```

time: 115 us -> 51.8 us (0.45)
  matrix products: 64.3 us -> 0 us
  Pallas kernels: 0 us -> 50.1 us
  waiting for transfers between devices: 26.9 us -> 0 us
  between operations: 13.5 us -> 0.01 us
  other arithmetic: 7.84 us -> 0 us
    dot_general x2 -> x0, matrix products: 64.3 us -> none  [einsum(): return jnp.einsum(form, a.astype(jnp.float32), b.astype(jnp.float32))]
    pallas_call x0 -> x1, Pallas kernels: none -> 50.1 us  [step(): pl.pallas_call(kernel, out_shape=jax.ShapeDtypeStruct((b, h, d), jnp.bflo...]
    all_gather x1 -> x0, waiting for transfers between devices: 26.9 us -> none  [step(): return together(lax.all_gather(part_of(q, k, v), 'sp')).reshape(q.shape)]
    reduce_sum x2 -> x0, other arithmetic: 4.24 us -> none  [the longest x1 2.27 us: together(): jnp.sum(total * scale, 0)]
    reduce_max x2 -> x0, other arithmetic: 1.76 us -> none  [the longest x1 1.64 us: together(): scale = jnp.exp(high - jnp.max(high, 0))]
    unnamed x0 -> x1, local copies, waits for them, and re-layouts: none -> 1.57 us
    mul x1 -> x0, local copies, waits for them, and re-layouts: 1.56 us -> none  [together(): seen * scale]
  transfers between devices with their start and end apart: 1 -> 0, of which waited for: 1 -> 0; matrix products, arithmetic and copies ran while one was open for 0% -> 0% of each run, Pallas kernels for 0% -> 0%
where the time goes in v1:
time: 51.8 us; the launch traced here: 51.7 us
  Pallas kernels  50.1 us (97%)
  local copies, waits for them, and re-layouts  1.57 us (3%)
    pallas_call x1, Pallas kernels, step(): pl.pallas_call(kernel, out_shape=jax.ShapeDtypeStruct((b, h, d), jnp.bflo...  50.1 us
    unnamed x1, local copies, waits for them, and re-layouts  1.57 us

profile of v1, /device:TPU:113, one launch (start us, length us, event | category | flops | bytes accessed | tf_op | source)
XLA Modules:
  0.0 51.7 jit_solution(2730517209677532945)
XLA Ops:
  0.0 50.1 %decode.1 = bf16[32,8,256]{2,1,0:T(8,128)(2,1)} custom-call(bf16[32,8,256]{2,1,0:T(8,128)(2,1)} %q_ref.1, bf16[32,4096,256]{2,1,0:T(8,128)(2,1)} %bitcast.k_ref, bf16[32,4096,256]{2,1,0:T(8,128)(2,1)} %bitcast.1.v_ref), custom_call_target="tpu_custom_call" | custom-call | tf_op jit(solution)/shard_map/decode/pallas_call | solution.py:185
  50.1 1.6 %copy.5 = bf16[32,8,256]{2,1,0:T(8,128)(2,1)} copy(bf16[32,8,256]{2,1,0:T(8,128)(2,1)} %decode.1) | data formatting | bytes 262144

commit v2 on v1

v2 whole, which is shorter than its diff:
```python
import functools

import jax
import jax.numpy as jnp
from jax import lax
from jax.experimental import pallas as pl
from jax.experimental.pallas import tpu as pltpu
from jax.sharding import PartitionSpec as P

SLOTS = 4
FLIGHT = 2 * (SLOTS - 1)
GROUP = 2
PIECES = 4
LIMIT = 32
MESH = pl.DeviceIdType.MESH


def iotas():
    return lax.broadcasted_iota(jnp.int32, (8, 128), 1), lax.broadcasted_iota(jnp.int32, (8, 128), 0)


def scores_of(q, k_ref):
    lane, sub = iotas()
    spread = jnp.concatenate([q] * 16, 0)
    full = lax.dot_general(k_ref[...], spread, (((1,), (1,)), ((), ())), preferred_element_type=jnp.float32)
    full = full.reshape(-1, 16, 8, 128)
    out = []
    for r in range(full.shape[0]):
        level = [full[r, i] for i in range(16)]
        bit = 8
        while len(level) > 1:
            level = [jnp.where((lane & bit) != 0, level[i + 1], level[i]) for i in range(0, len(level), 2)]
            bit *= 2
        out.append(jnp.sum(jnp.where((lane & 7) == sub, level[0], 0.0), 0, keepdims=True))
    return jnp.concatenate(out, 0)


def fold(x, op):
    turned = [x] + [pltpu.roll(x, s, 1) for s in range(8, 128, 8)]
    while len(turned) > 1:
        turned = [op(turned[i], turned[i + 1]) for i in range(0, len(turned), 2)]
    return turned[0]


def kernel(q_hbm, k_ref, v_ref, o_ref, q_ref, k_buf, v_buf, gathered, sums, q_sem, k_sem, v_sem, last_sem, send_sem, recv_sem, send_sum, recv_sum):
    batch = k_ref.shape[0]
    n = lax.axis_size("sp")
    me = lax.axis_index("sp")
    lane, sub = iotas()
    diag = (lane & 7) == sub

    def k_copy(b, slot):
        return pltpu.make_async_copy(k_ref.at[b], k_buf.at[slot], k_sem.at[slot])

    def last_copy(piece):
        rows = v_ref.shape[1] // PIECES
        part = pl.ds(piece * rows, rows)
        return pltpu.make_async_copy(v_ref.at[batch - 1, part], v_buf.at[(batch - 1) % SLOTS, part], last_sem.at[piece])

    def v_copy(b, slot):
        return pltpu.make_async_copy(v_ref.at[b], v_buf.at[slot], v_sem.at[slot])

    q_copy = pltpu.make_async_copy(q_hbm, q_ref, q_sem)
    def start(i):
        if i == 0 or i % 2:
            b = 0 if i == 0 else (i + 1) // 2
            k_copy(b, b % SLOTS).start()
        else:
            b = (i - 2) // 2
            v_copy(b, b % SLOTS).start()

    q_copy.start()
    start(0)
    q_copy.wait()
    for i in range(1, FLIGHT):
        start(i)

    barrier = pltpu.get_barrier_semaphore()
    for step in range(1, n):
        pl.semaphore_signal(barrier, inc=1, device_id={"sp": lax.rem(me + step, n)}, device_id_type=MESH)

    def score(b, slot):
        return scores_of(q_ref[b], k_buf.at[slot]) * k_ref.shape[2] ** -0.5

    def soften(s):
        high = fold(jnp.max(s, 0, keepdims=True), jnp.maximum)
        p = jnp.exp(s - high)
        total = fold(jnp.sum(p, 0, keepdims=True), jnp.add)
        return p, jnp.where(lane[:1] < 64, high, total)

    def weigh(p, v):
        big = [jnp.where(diag, jnp.broadcast_to(p[r:r + 1], (8, 128)), 0.0) for r in range(p.shape[0])]
        return jnp.dot(jnp.concatenate(big, 1).astype(jnp.bfloat16), v, preferred_element_type=jnp.float32)

    steps = sorted(range(1, n), key=lambda step: -min(step, n - step))

    def part_copy(first, count, which, owner, step):
        block = gathered.at[owner, pl.ds(first, count)]
        return pltpu.make_async_remote_copy(block, block, send_sem.at[which, step], recv_sem.at[which, owner], device_id={"sp": lax.rem(me + step, n)}, device_id_type=MESH)

    def sum_copy(first, count, which, owner, step):
        block = sums.at[owner, pl.ds(first, count)]
        return pltpu.make_async_remote_copy(block, block, send_sum.at[which, step], recv_sum.at[which, owner], device_id={"sp": lax.rem(me + step, n)}, device_id_type=MESH)

    def send(copy, *which):
        for step in steps:
            copy(*which, me, step).start()

    def received(copy, *which):
        for step in steps:
            copy(*which, lax.rem(me + step, n), step).wait_recv()

    def sent(copy, *which):
        for step in steps:
            copy(*which, me, step).wait_send()

    def shares(b):
        rows = jnp.concatenate([sums[d, b] for d in range(n)], 0)
        high = jnp.max(rows, 0, keepdims=True)
        scale = jnp.exp(rows - high)
        total = jnp.sum(pltpu.roll(rows, 64, 1) * scale, 0, keepdims=True)
        scale = scale / total
        return [jnp.sum(jnp.where(lane == sub, jnp.broadcast_to(scale[d:d + 1], (8, 128)), 0.0), 1, keepdims=True) for d in range(n)]

    def combine(b, columns):
        result = [gathered[d, b].astype(jnp.float32) * columns[d] for d in range(n)]
        while len(result) > 1:
            result = [result[i] + result[i + 1] for i in range(0, len(result), 2)]
        o_ref[b] = result[0].astype(o_ref.dtype)

    main = batch - 2

    k_copy(0, 0).wait()
    start(FLIGHT)
    s0 = score(0, 0)
    k_copy(1, 1).wait()
    start(FLIGHT + 1)
    p0, row = soften(s0)
    s1 = score(1, 1)
    sums[me, 0] = row
    pl.semaphore_wait(barrier, n - 1)

    def body(b, carry):
        s, p = carry
        ahead = SLOTS - 1
        slot, k_slot = lax.rem(b, SLOTS), lax.rem(b + 2, SLOTS)
        v_copy(b, slot).wait()
        k_copy(b + 2, k_slot).wait()

        @pl.when(b + ahead < batch - 1)
        def _():
            v_copy(b + ahead, lax.rem(b + ahead, SLOTS)).start()

        @pl.when(b + ahead == batch - 1)
        def _():
            for piece in range(PIECES):
                last_copy(piece).start()

        @pl.when(b + 2 + ahead < batch)
        def _():
            k_copy(b + 2 + ahead, lax.rem(b + 2 + ahead, SLOTS)).start()

        gathered[me, b] = weigh(p, v_buf[slot]).astype(jnp.bfloat16)
        s_next = score(b + 2, k_slot)
        p_next, row = soften(s)
        sums[me, b + 1] = row

        @pl.when(lax.rem(b, GROUP) == GROUP - 1)
        def _():
            send(part_copy, b - (GROUP - 1), GROUP, 0)
            send(sum_copy, b - (GROUP - 1), GROUP, 0)

        return s_next, p_next

    s, p = lax.fori_loop(0, batch - 2, body, (s1, p0))
    last = batch - 1
    v_copy(main, main % SLOTS).wait()
    gathered[me, main] = weigh(p, v_buf[main % SLOTS]).astype(jnp.bfloat16)
    p, row = soften(s)
    sums[me, last] = row
    send(sum_copy, main, 2, 1)
    send(part_copy, main, 1, 1)
    rows, tokens = p.shape[0] // PIECES, v_buf.shape[1] // PIECES
    result = 0.0
    for piece in range(PIECES):
        last_copy(piece).wait()
        result += weigh(p[piece * rows:(piece + 1) * rows], v_buf[last % SLOTS, piece * tokens:(piece + 1) * tokens])
    gathered[me, last] = result.astype(jnp.bfloat16)
    send(part_copy, last, 1, 2)

    received(sum_copy, 0, main, 0)
    received(part_copy, 0, main, 0)

    def finish(i, _):
        columns = [shares(i * 5 + j) for j in range(5)]
        for j in range(5):
            combine(i * 5 + j, columns[j])
        return 0

    lax.fori_loop(0, main // 5, finish, 0)
    received(sum_copy, main, 2, 1)
    columns = [shares(main), shares(last)]
    received(part_copy, main, 1, 1)
    combine(main, columns[0])
    received(part_copy, last, 1, 2)
    combine(last, columns[1])
    sent(sum_copy, 0, main, 0)
    sent(part_copy, 0, main, 0)
    sent(sum_copy, main, 2, 1)
    sent(part_copy, main, 1, 1)
    sent(part_copy, last, 1, 2)


def solution(mesh):
    n = mesh.shape["sp"]

    def step(q, k, v):
        b, u, h, d = k.shape
        rows = u * h
        return pl.pallas_call(
            kernel,
            out_shape=jax.ShapeDtypeStruct((b, h, d), jnp.bfloat16),
            in_specs=[pl.BlockSpec(memory_space=pltpu.HBM)] * 3,
            out_specs=pl.BlockSpec(memory_space=pltpu.VMEM),
            scratch_shapes=[
                pltpu.VMEM((b, h, d), jnp.bfloat16),
                pltpu.VMEM((SLOTS, rows, d), jnp.bfloat16),
                pltpu.VMEM((SLOTS, rows, d), jnp.bfloat16),
                pltpu.VMEM((n, b, h, d), jnp.bfloat16),
                pltpu.VMEM((n, b, 1, 128), jnp.float32),
                pltpu.SemaphoreType.DMA,
                pltpu.SemaphoreType.DMA((SLOTS,)),
                pltpu.SemaphoreType.DMA((SLOTS,)),
                pltpu.SemaphoreType.DMA((PIECES,)),
                pltpu.SemaphoreType.DMA((3, n)),
                pltpu.SemaphoreType.DMA((3, n)),
                pltpu.SemaphoreType.DMA((3, n)),
                pltpu.SemaphoreType.DMA((3, n)),
            ],
            name="decode",
            compiler_params=pltpu.CompilerParams(collective_id=0, has_side_effects=True, vmem_limit_bytes=LIMIT << 20),
        )(pltpu.with_memory_space_constraint(q, pltpu.HBM), k.reshape(b, rows, d), v.reshape(b, rows, d))

    return jax.shard_map(
        step,
        mesh=mesh,
        in_specs=(P("dp", None, None), P("dp", "sp", None, None), P("dp", "sp", None, None)),
        out_specs=P("dp", None, None),
        check_vma=False,
    )
```

time: 51.8 us -> 49.6 us (0.958)
  Pallas kernels: 50.1 us -> 48.9 us
  local copies, waits for them, and re-layouts: 1.57 us -> 0.66 us
    pallas_call x1, Pallas kernels: 50.1 us -> 48.9 us  [step(): pl.pallas_call(kernel, out_shape=jax.ShapeDtypeStruct((b, h, d), jnp.bflo...]
    unnamed x1, local copies, waits for them, and re-layouts: 1.57 us -> 0.66 us
where the time goes in v2:
time: 49.6 us; the launch traced here: 49.5 us
  Pallas kernels  48.9 us (99%)
  local copies, waits for them, and re-layouts  0.66 us (1%)
    pallas_call x1, Pallas kernels, step(): pl.pallas_call(kernel, out_shape=jax.ShapeDtypeStruct((b, h, d), jnp.bflo...  48.9 us

profile of v2, /device:TPU:113, one launch (start us, length us, event | category | flops | bytes accessed | tf_op | source)
XLA Modules:
  0.0 49.5 jit_solution(1947749150209145927)
XLA Ops:
  0.0 48.9 %decode.1 = bf16[32,8,256]{2,1,0:T(8,128)(2,1)S(1)} custom-call(bf16[32,8,256]{2,1,0:T(8,128)(2,1)} %q_hbm.1, bf16[32,4096,256]{2,1,0:T(8,128)(2,1)} %bitcast.k_ref, bf16[32,4096,256]{2,1,0:T(8,128)(2,1)} %bitcast.1.v_ref), custom_call_target="tpu_custom_call" | custom-call | tf_op jit(solution)/shard_map/decode/pallas_call | solution.py:220
  48.9 0.7 %copy.5 = bf16[32,8,256]{2,1,0:T(8,128)(2,1)} copy(bf16[32,8,256]{2,1,0:T(8,128)(2,1)S(1)} %decode.1) | data formatting | bytes 262144

commit v3 on v0

v3 whole, which is shorter than its diff:
```python
import functools

import jax
import jax.numpy as jnp
from jax import lax
from jax.experimental import pallas as pl
from jax.experimental.pallas import tpu as pltpu
from jax.sharding import PartitionSpec as P

LEAD = 4
AHEAD = 3
SLOTS = AHEAD + 1
GROUP = 2
PIECES = 2
LIMIT = 32
MESH = pl.DeviceIdType.MESH


def iotas():
    return lax.broadcasted_iota(jnp.int32, (8, 128), 1), lax.broadcasted_iota(jnp.int32, (8, 128), 0)


def scores_of(q, k_ref):
    lane, sub = iotas()
    spread = jnp.concatenate([q] * 16, 0)
    full = lax.dot_general(k_ref[...], spread, (((1,), (1,)), ((), ())), preferred_element_type=jnp.float32)
    full = full.reshape(-1, 16, 8, 128)
    out = []
    for r in range(full.shape[0]):
        level = [full[r, i] for i in range(16)]
        bit = 8
        while len(level) > 1:
            level = [jnp.where((lane & bit) != 0, level[i + 1], level[i]) for i in range(0, len(level), 2)]
            bit *= 2
        out.append(jnp.sum(jnp.where((lane & 7) == sub, level[0], 0.0), 0, keepdims=True))
    return jnp.concatenate(out, 0)


def fold(x, op):
    turned = [x] + [pltpu.roll(x, s, 1) for s in range(8, 128, 8)]
    while len(turned) > 1:
        turned = [op(turned[i], turned[i + 1]) for i in range(0, len(turned), 2)]
    return turned[0]


def kernel(q_hbm, k_ref, v_ref, o_ref, q_ref, k_buf, v_buf, weights, gathered, sums, q_sem, k_sem, v_sem, send_sem, recv_sem, send_sum, recv_sum):
    batch = k_ref.shape[0]
    n = lax.axis_size("sp")
    me = lax.axis_index("sp")
    lane, sub = iotas()
    diag = (lane & 7) == sub

    last, main = batch - 1, batch - LEAD

    def k_copy(b):
        slot = lax.rem(b, SLOTS)
        return pltpu.make_async_copy(k_ref.at[b], k_buf.at[slot], k_sem.at[slot])

    tokens = v_ref.shape[1] // PIECES

    def v_copy(b, piece):
        slot, part = lax.rem(b, SLOTS), pl.ds(pl.multiple_of(piece * tokens, tokens), tokens)
        return pltpu.make_async_copy(v_ref.at[b, part], v_buf.at[slot, part], v_sem.at[slot, piece])

    def v_start(b):
        for piece in range(PIECES):
            v_copy(b, piece).start()

    q_copy = pltpu.make_async_copy(q_hbm, q_ref, q_sem)
    q_copy.start()
    k_copy(0).start()

    barrier = pltpu.get_barrier_semaphore()
    for step in range(1, n):
        pl.semaphore_signal(barrier, inc=1, device_id={"sp": lax.rem(me + step, n)}, device_id_type=MESH)

    def score(b):
        return scores_of(q_ref[b], k_buf.at[lax.rem(b, SLOTS)]) * k_ref.shape[2] ** -0.5

    def soften(b, s):
        high = fold(jnp.max(s, 0, keepdims=True), jnp.maximum)
        p = jnp.exp(s - high)
        total = fold(jnp.sum(p, 0, keepdims=True), jnp.add)
        weights[lax.rem(b, LEAD)] = p
        sums[me, b] = jnp.where(lane[:1] < 64, high, total)

    def weigh(p, v):
        big = [jnp.where(diag, jnp.broadcast_to(p[r:r + 1], (8, 128)), 0.0) for r in range(p.shape[0])]
        return jnp.dot(jnp.concatenate(big, 1).astype(jnp.bfloat16), v, preferred_element_type=jnp.float32)

    steps = sorted(range(1, n), key=lambda step: -min(step, n - step))

    def send(array, send_sem, recv_sem, first, count, which):
        block = array.at[me, pl.ds(first, count)]
        for step in steps:
            pltpu.make_async_remote_copy(block, block, send_sem.at[which], recv_sem.at[which], device_id={"sp": lax.rem(me + step, n)}, device_id_type=MESH).start()

    def everyone(array, send_sem, recv_sem, first, count, which):
        block = array.at[pl.ds(0, n - 1), pl.ds(first, count)]
        return pltpu.make_async_remote_copy(block, block, send_sem.at[which], recv_sem.at[which], device_id={"sp": lax.rem(me + 1, n)}, device_id_type=MESH)

    parts, part_sums = (gathered, send_sem, recv_sem), (sums, send_sum, recv_sum)

    def shares(b):
        rows = jnp.concatenate([sums[d, b] for d in range(n)], 0)
        high = jnp.max(rows, 0, keepdims=True)
        scale = jnp.exp(rows - high)
        total = jnp.sum(pltpu.roll(rows, 64, 1) * scale, 0, keepdims=True)
        scale = scale / total
        return [jnp.sum(jnp.where(lane == sub, jnp.broadcast_to(scale[d:d + 1], (8, 128)), 0.0), 1, keepdims=True) for d in range(n)]

    def combine(b, columns):
        result = [gathered[d, b].astype(jnp.float32) * columns[d] for d in range(n)]
        while len(result) > 1:
            result = [result[i] + result[i + 1] for i in range(0, len(result), 2)]
        o_ref[b] = result[0].astype(o_ref.dtype)

    q_copy.wait()
    for b in range(1, AHEAD):
        k_copy(b).start()

    def open_up(b, s):
        k_copy(b).wait()
        k_copy(b + AHEAD).start()

        @pl.when(b < AHEAD)
        def _():
            v_start(b)

        s_next = score(b)
        soften(jnp.maximum(b - 1, 0), s)
        return s_next

    s = lax.fori_loop(0, LEAD, open_up, jnp.zeros(weights.shape[1:], jnp.float32))
    pl.semaphore_wait(barrier, n - 1)

    def body(b, s):
        for piece in range(PIECES):
            v_copy(b, piece).wait()
        k_copy(b + LEAD).wait()
        v_start(b + AHEAD)

        @pl.when(b + LEAD + AHEAD < batch)
        def _():
            k_copy(b + LEAD + AHEAD).start()

        gathered[me, b] = weigh(weights[lax.rem(b, LEAD)], v_buf[lax.rem(b, SLOTS)]).astype(jnp.bfloat16)
        s_next = score(b + LEAD)
        soften(b + LEAD - 1, s)

        @pl.when(lax.rem(b, GROUP) == GROUP - 1)
        def _():
            send(*parts, b - (GROUP - 1), GROUP, 0)
            send(*part_sums, b - (GROUP - 1), GROUP, 0)

        return s_next

    s = lax.fori_loop(0, main, body, s)
    soften(last, s)
    send(*part_sums, main, LEAD, 1)

    def close_down(i, result):
        b, piece = main + i // PIECES, lax.rem(i, PIECES)
        v_copy(b, piece).wait()

        @pl.when((piece == 0) & (b + AHEAD < batch))
        def _():
            v_start(b + AHEAD)

        slot, rows = lax.rem(b, SLOTS), weights.shape[1] // PIECES
        p = weights[lax.rem(b, LEAD), pl.ds(pl.multiple_of(piece * rows, rows), rows)]
        v = v_buf[slot, pl.ds(pl.multiple_of(piece * tokens, tokens), tokens)]
        result = jnp.where(piece == 0, 0.0, result) + weigh(p, v)

        @pl.when(piece == PIECES - 1)
        def _():
            gathered[me, b] = result.astype(jnp.bfloat16)
            send(*parts, b, 1, 1 + i // PIECES)

        return result

    lax.fori_loop(0, LEAD * PIECES, close_down, jnp.zeros(o_ref.shape[1:], jnp.float32))

    everyone(*part_sums, 0, main, 0).wait_recv()
    everyone(*parts, 0, main, 0).wait_recv()

    def finish(i, _):
        columns = [shares(i * 4 + j) for j in range(4)]
        for j in range(4):
            combine(i * 4 + j, columns[j])
        return 0

    lax.fori_loop(0, main // 4, finish, 0)
    everyone(*part_sums, 0, main, 0).wait_send()
    everyone(*parts, 0, main, 0).wait_send()
    everyone(*part_sums, main, LEAD, 1).wait_send()
    everyone(*part_sums, main, LEAD, 1).wait_recv()

    def finish_last(i, _):
        columns = shares(main + i)
        everyone(*parts, main + i, 1, 1 + i).wait_send()
        everyone(*parts, main + i, 1, 1 + i).wait_recv()
        combine(main + i, columns)
        return 0

    lax.fori_loop(0, LEAD, finish_last, 0)


def solution(mesh):
    n = mesh.shape["sp"]

    def step(q, k, v):
        b, u, h, d = k.shape
        rows = u * h
        return pl.pallas_call(
            kernel,
            out_shape=jax.ShapeDtypeStruct((b, h, d), jnp.bfloat16),
            in_specs=[pl.BlockSpec(memory_space=pltpu.HBM)] * 3,
            out_specs=pl.BlockSpec(memory_space=pltpu.VMEM),
            scratch_shapes=[
                pltpu.VMEM((b, h, d), jnp.bfloat16),
                pltpu.VMEM((SLOTS, rows, d), jnp.bfloat16),
                pltpu.VMEM((SLOTS, rows, d), jnp.bfloat16),
                pltpu.VMEM((LEAD, rows // 128, 128), jnp.float32),
                pltpu.VMEM((n, b, h, d), jnp.bfloat16),
                pltpu.VMEM((n, b, 1, 128), jnp.float32),
                pltpu.SemaphoreType.DMA,
                pltpu.SemaphoreType.DMA((SLOTS,)),
                pltpu.SemaphoreType.DMA((SLOTS, PIECES)),
                pltpu.SemaphoreType.DMA((LEAD + 1,)),
                pltpu.SemaphoreType.DMA((LEAD + 1,)),
                pltpu.SemaphoreType.DMA((LEAD + 1,)),
                pltpu.SemaphoreType.DMA((LEAD + 1,)),
            ],
            name="decode",
            compiler_params=pltpu.CompilerParams(collective_id=0, has_side_effects=True, vmem_limit_bytes=LIMIT << 20),
        )(pltpu.with_memory_space_constraint(q, pltpu.HBM), k.reshape(b, rows, d), v.reshape(b, rows, d))

    return jax.shard_map(
        step,
        mesh=mesh,
        in_specs=(P("dp", None, None), P("dp", "sp", None, None), P("dp", "sp", None, None)),
        out_specs=P("dp", None, None),
        check_vma=False,
    )
```

time: 115 us -> 48.4 us (0.42)
  matrix products: 64.3 us -> 0 us
  Pallas kernels: 0 us -> 47.6 us
  waiting for transfers between devices: 26.9 us -> 0 us
  between operations: 13.5 us -> 0.01 us
  other arithmetic: 7.84 us -> 0 us
  local copies, waits for them, and re-layouts: 2.1 us -> 0.66 us
    dot_general x2 -> x0, matrix products: 64.3 us -> none  [einsum(): return jnp.einsum(form, a.astype(jnp.float32), b.astype(jnp.float32))]
    pallas_call x0 -> x1, Pallas kernels: none -> 47.6 us  [step(): pl.pallas_call(kernel, out_shape=jax.ShapeDtypeStruct((b, h, d), jnp.bflo...]
    all_gather x1 -> x0, waiting for transfers between devices: 26.9 us -> none  [step(): return together(lax.all_gather(part_of(q, k, v), 'sp')).reshape(q.shape)]
    reduce_sum x2 -> x0, other arithmetic: 4.24 us -> none  [the longest x1 2.27 us: together(): jnp.sum(total * scale, 0)]
    reduce_max x2 -> x0, other arithmetic: 1.76 us -> none  [the longest x1 1.64 us: together(): scale = jnp.exp(high - jnp.max(high, 0))]
    mul x1 -> x0, local copies, waits for them, and re-layouts: 1.56 us -> none  [together(): seen * scale]
  transfers between devices with their start and end apart: 1 -> 0, of which waited for: 1 -> 0; matrix products, arithmetic and copies ran while one was open for 0% -> 0% of each run, Pallas kernels for 0% -> 0%
where the time goes in v3:
time: 48.4 us; the launch traced here: 48.3 us
  Pallas kernels  47.6 us (98%)
  local copies, waits for them, and re-layouts  0.66 us (1%)
    pallas_call x1, Pallas kernels, step(): pl.pallas_call(kernel, out_shape=jax.ShapeDtypeStruct((b, h, d), jnp.bflo...  47.6 us

profile of v3, /device:TPU:113, one launch (start us, length us, event | category | flops | bytes accessed | tf_op | source)
XLA Modules:
  0.0 48.3 jit_solution(8352334461345932766)
XLA Ops:
  0.0 47.6 %decode.1 = bf16[32,8,256]{2,1,0:T(8,128)(2,1)S(1)} custom-call(bf16[32,8,256]{2,1,0:T(8,128)(2,1)} %q_hbm.1, bf16[32,4096,256]{2,1,0:T(8,128)(2,1)} %bitcast.k_ref, bf16[32,4096,256]{2,1,0:T(8,128)(2,1)} %bitcast.1.v_ref), custom_call_target="tpu_custom_call" | custom-call | tf_op jit(solution)/shard_map/decode/pallas_call | solution.py:215
  47.6 0.7 %copy.5 = bf16[32,8,256]{2,1,0:T(8,128)(2,1)} copy(bf16[32,8,256]{2,1,0:T(8,128)(2,1)S(1)} %decode.1) | data formatting | bytes 262144

commit v4 on v3

--- a/solution.py
+++ b/solution.py
@@ -11,7 +11,7 @@
 AHEAD = 3
 SLOTS = AHEAD + 1
 GROUP = 2
-PIECES = 2
+PIECES = 1
 LIMIT = 32
 MESH = pl.DeviceIdType.MESH
 
@@ -156,16 +156,13 @@
         return s_next
 
     s = lax.fori_loop(0, main, body, s)
+    v_start(last)
     soften(last, s)
     send(*part_sums, main, LEAD, 1)
 
     def close_down(i, result):
         b, piece = main + i // PIECES, lax.rem(i, PIECES)
         v_copy(b, piece).wait()
-
-        @pl.when((piece == 0) & (b + AHEAD < batch))
-        def _():
-            v_start(b + AHEAD)
 
         slot, rows = lax.rem(b, SLOTS), weights.shape[1] // PIECES
         p = weights[lax.rem(b, LEAD), pl.ds(pl.multiple_of(piece * rows, rows), rows)]

time: 48.4 us -> 48.1 us (level)
  no operation moved by 1% of the time
where the time goes in v4:
time: 48.1 us; the launch traced here: 48 us
  Pallas kernels  47.3 us (98%)
  local copies, waits for them, and re-layouts  0.66 us (1%)
    pallas_call x1, Pallas kernels, step(): pl.pallas_call(kernel, out_shape=jax.ShapeDtypeStruct((b, h, d), jnp.bflo...  47.3 us

profile of v4, /device:TPU:113, one launch (start us, length us, event | category | flops | bytes accessed | tf_op | source)
XLA Modules:
  0.0 48.0 jit_solution(17166436487130182410)
XLA Ops:
  0.0 47.3 %decode.1 = bf16[32,8,256]{2,1,0:T(8,128)(2,1)S(1)} custom-call(bf16[32,8,256]{2,1,0:T(8,128)(2,1)} %q_hbm.1, bf16[32,4096,256]{2,1,0:T(8,128)(2,1)} %bitcast.k_ref, bf16[32,4096,256]{2,1,0:T(8,128)(2,1)} %bitcast.1.v_ref), custom_call_target="tpu_custom_call" | custom-call | tf_op jit(solution)/shard_map/decode/pallas_call | solution.py:212
  47.4 0.7 %copy.5 = bf16[32,8,256]{2,1,0:T(8,128)(2,1)} copy(bf16[32,8,256]{2,1,0:T(8,128)(2,1)S(1)} %decode.1) | data formatting | bytes 262144

commit v5 on v4

--- a/solution.py
+++ b/solution.py
@@ -69,6 +69,8 @@
     q_copy = pltpu.make_async_copy(q_hbm, q_ref, q_sem)
     q_copy.start()
     k_copy(0).start()
+    k_copy(1).start(priority=1)
+    k_copy(2).start(priority=1)
 
     barrier = pltpu.get_barrier_semaphore()
     for step in range(1, n):
@@ -116,8 +118,6 @@
         o_ref[b] = result[0].astype(o_ref.dtype)
 
     q_copy.wait()
-    for b in range(1, AHEAD):
-        k_copy(b).start()
 
     def open_up(b, s):
         k_copy(b).wait()

time: 48.1 us -> 47.8 us (level)
  no operation moved by 1% of the time
where the time goes in v5:
time: 47.8 us; the launch traced here: 47.7 us
  Pallas kernels  47.1 us (99%)
  local copies, waits for them, and re-layouts  0.66 us (1%)
    pallas_call x1, Pallas kernels, step(): pl.pallas_call(kernel, out_shape=jax.ShapeDtypeStruct((b, h, d), jnp.bflo...  47.1 us

profile of v5, /device:TPU:113, one launch (start us, length us, event | category | flops | bytes accessed | tf_op | source)
XLA Modules:
  0.0 47.7 jit_solution(5017549485159653563)
XLA Ops:
  0.0 47.1 %decode.1 = bf16[32,8,256]{2,1,0:T(8,128)(2,1)S(1)} custom-call(bf16[32,8,256]{2,1,0:T(8,128)(2,1)} %q_hbm.1, bf16[32,4096,256]{2,1,0:T(8,128)(2,1)} %bitcast.k_ref, bf16[32,4096,256]{2,1,0:T(8,128)(2,1)} %bitcast.1.v_ref), custom_call_target="tpu_custom_call" | custom-call | tf_op jit(solution)/shard_map/decode/pallas_call | solution.py:212
  47.1 0.7 %copy.5 = bf16[32,8,256]{2,1,0:T(8,128)(2,1)} copy(bf16[32,8,256]{2,1,0:T(8,128)(2,1)S(1)} %decode.1) | data formatting | bytes 262144

commit v6 on v5

--- a/solution.py
+++ b/solution.py
@@ -11,6 +11,7 @@
 AHEAD = 3
 SLOTS = AHEAD + 1
 GROUP = 2
+SUMS = 8
 PIECES = 1
 LIMIT = 32
 MESH = pl.DeviceIdType.MESH
@@ -151,14 +152,17 @@
         @pl.when(lax.rem(b, GROUP) == GROUP - 1)
         def _():
             send(*parts, b - (GROUP - 1), GROUP, 0)
-            send(*part_sums, b - (GROUP - 1), GROUP, 0)
+
+        @pl.when(lax.rem(b, SUMS) == SUMS - 1)
+        def _():
+            send(*part_sums, b - (SUMS - 1), SUMS, 0)
 
         return s_next
 
     s = lax.fori_loop(0, main, body, s)
     v_start(last)
     soften(last, s)
-    send(*part_sums, main, LEAD, 1)
+    send(*part_sums, batch - SUMS, SUMS, 1)
 
     def close_down(i, result):
         b, piece = main + i // PIECES, lax.rem(i, PIECES)
@@ -178,20 +182,23 @@
 
     lax.fori_loop(0, LEAD * PIECES, close_down, jnp.zeros(o_ref.shape[1:], jnp.float32))
 
-    everyone(*part_sums, 0, main, 0).wait_recv()
+    everyone(*part_sums, 0, batch - SUMS, 0).wait_recv()
     everyone(*parts, 0, main, 0).wait_recv()
 
     def finish(i, _):
+        @pl.when(i == (batch - SUMS) // 4)
+        def _():
+            everyone(*part_sums, batch - SUMS, SUMS, 1).wait_recv()
+
         columns = [shares(i * 4 + j) for j in range(4)]
         for j in range(4):
             combine(i * 4 + j, columns[j])
         return 0
 
     lax.fori_loop(0, main // 4, finish, 0)
-    everyone(*part_sums, 0, main, 0).wait_send()
+    everyone(*part_sums, 0, batch - SUMS, 0).wait_send()
     everyone(*parts, 0, main, 0).wait_send()
-    everyone(*part_sums, main, LEAD, 1).wait_send()
-    everyone(*part_sums, main, LEAD, 1).wait_recv()
+    everyone(*part_sums, batch - SUMS, SUMS, 1).wait_send()
 
     def finish_last(i, _):
         columns = shares(main + i)

time: 47.8 us -> 47.6 us (level)
  no operation moved by 1% of the time
where the time goes in v6:
time: 47.6 us; the launch traced here: 47.5 us
  Pallas kernels  46.8 us (98%)
  local copies, waits for them, and re-layouts  0.66 us (1%)
    pallas_call x1, Pallas kernels, step(): pl.pallas_call(kernel, out_shape=jax.ShapeDtypeStruct((b, h, d), jnp.bflo...  46.8 us

profile of v6, /device:TPU:113, one launch (start us, length us, event | category | flops | bytes accessed | tf_op | source)
XLA Modules:
  0.0 47.5 jit_solution(3771827838157808874)
XLA Ops:
  0.0 46.8 %decode.1 = bf16[32,8,256]{2,1,0:T(8,128)(2,1)S(1)} custom-call(bf16[32,8,256]{2,1,0:T(8,128)(2,1)} %q_hbm.1, bf16[32,4096,256]{2,1,0:T(8,128)(2,1)} %bitcast.k_ref, bf16[32,4096,256]{2,1,0:T(8,128)(2,1)} %bitcast.1.v_ref), custom_call_target="tpu_custom_call" | custom-call | tf_op jit(solution)/shard_map/decode/pallas_call | solution.py:219
  46.8 0.7 %copy.5 = bf16[32,8,256]{2,1,0:T(8,128)(2,1)} copy(bf16[32,8,256]{2,1,0:T(8,128)(2,1)S(1)} %decode.1) | data formatting | bytes 262144
